TPU v7x, 32 devices: a whole 2x2x4 slice. The times are simulated.
32 devices in a mesh: tensor: 4 (over z), dp: 8 (over y, x, core).
Axes of the slice: x: 2, y: 2, z: 4, core: 2. Of those that a mesh axis runs over, the one named last changes fastest.
Arguments:
- grads: bfloat16 [8, 40, 28672], P('dp', None, 'tensor'), may hold values from -6 to 6
- offload_mask: int32 [8, 5], replicated, may hold values from 0 to 1, as said below
- owner_map: int32 [8], replicated, may hold values from 0 to 7, as said below
- local_master: float32 [24, 28672], P('dp', 'tensor'), may hold values from -6 to 6
- local_moment: float32 [24, 28672], P('dp', 'tensor'), may hold values from -1.2 to 1.2
- local_second: float32 [24, 28672], P('dp', 'tensor'), may hold values from 0.001 to 0.1
- offload_master: float32 [16, 2, 28672], P('dp', None, 'tensor'), may hold values from -6 to 6
- offload_moment: float32 [16, 2, 28672], P('dp', None, 'tensor'), may hold values from -1.2 to 1.2
- offload_second: float32 [16, 2, 28672], P('dp', None, 'tensor'), may hold values from 0.001 to 0.1
Outputs:
- new_weights: bfloat16 [40, 28672], P(None, 'tensor')
- grad_norm: float32 [], replicated
- new_local_master: float32 [24, 28672], P('dp', 'tensor')
- new_local_moment: float32 [24, 28672], P('dp', 'tensor')
- new_local_second: float32 [24, 28672], P('dp', 'tensor')
- new_offload_master: float32 [16, 2, 28672], P('dp', None, 'tensor')
- new_offload_moment: float32 [16, 2, 28672], P('dp', None, 'tensor')
- new_offload_second: float32 [16, 2, 28672], P('dp', None, 'tensor')
Inputs may be any that keep to these rules, and one draw needn't show every extreme that they name: Each row of offload_mask holds exactly 2 ones. `owner_map`: no device is named by more than 2 shards, and some device is named by exactly 2.
All inputs are finite; a program needn't handle non-finite values.
Results may differ from a plain program's by a relative error of at most 0.0039.
Values may be sent and summed in bfloat16 or wider, within the bound.
A program may use at most 128 MiB of HBM per device.

v0:
```python
import jax
import jax.numpy as jnp
from jax import lax
from jax.sharding import PartitionSpec as P

beta_first = 0.9
beta_second = 0.95
learn_rate = 0.02
decay_rate = 0.1
epsilon_value = 1e-08
step_count = 10
bias_first = 1.0 - beta_first**step_count
bias_second = 1.0 - beta_second**step_count


def adam_update(master, moment, second, gradient):
    moment_new = beta_first * moment + (1.0 - beta_first) * gradient
    second_new = beta_second * second + (1.0 - beta_second) * gradient * gradient
    scaled = moment_new / bias_first / (jnp.sqrt(second_new / bias_second) + epsilon_value)
    master_new = master - learn_rate * (scaled + decay_rate * master)
    return (master_new, moment_new, second_new)


def row_tables(offload_mask, owner_map):
    shards = owner_map.shape[0]
    row_dev = offload_mask.shape[1]
    numbers = jnp.arange(shards, dtype=jnp.int32)
    same_owner = owner_map[:, None] == owner_map[None, :]
    earlier = numbers[None, :] < numbers[:, None]
    slot_of = jnp.sum((same_owner & earlier).astype(jnp.int32), axis=1)
    off_rank = jnp.cumsum(offload_mask, axis=1) - offload_mask
    keep_rank = jnp.arange(row_dev, dtype=jnp.int32)[None, :] - off_rank
    return (slot_of, off_rank, keep_rank)


def body(
    grads,
    offload_mask,
    owner_map,
    local_master,
    local_moment,
    local_second,
    offload_master,
    offload_moment,
    offload_second,
):
    devices = lax.axis_size("dp")
    position = lax.axis_index("dp")
    row_dev = offload_mask.shape[1]
    kept_count = local_master.shape[0]
    slot_count = offload_master.shape[0]
    offloaded = offload_master.shape[1]
    columns = grads.shape[2]
    slot_of, off_rank, keep_rank = row_tables(offload_mask, owner_map)
    is_off = offload_mask == 1
    row_range = jnp.arange(row_dev, dtype=jnp.int32)[None, None, :]
    off_hits = is_off[:, None, :] & (
        off_rank[:, None, :] == jnp.arange(offloaded, dtype=jnp.int32)[None, :, None]
    )
    off_index = jnp.sum(jnp.where(off_hits, row_range, 0), axis=2)
    keep_hits = ~is_off[:, None, :] & (
        keep_rank[:, None, :] == jnp.arange(kept_count, dtype=jnp.int32)[None, :, None]
    )
    keep_index = jnp.sum(jnp.where(keep_hits, row_range, 0), axis=2)
    shard_numbers = jnp.arange(devices, dtype=jnp.int32)
    matches = (owner_map[None, None, :] == shard_numbers[:, None, None]) & (
        slot_of[None, None, :] == jnp.arange(slot_count, dtype=jnp.int32)[None, :, None]
    )
    source_of = jnp.sum(jnp.where(matches, shard_numbers[None, None, :], 0), axis=2)
    filled = jnp.any(matches, axis=2)
    my_filled = jnp.take(filled, position, axis=0)
    local_grads = grads[0]
    keep_rows = shard_numbers[:, None] * row_dev + keep_index
    slot_rows = source_of[:, :, None] * row_dev + jnp.take(off_index, source_of, axis=0)
    row_table = jnp.concatenate(
        [keep_rows, slot_rows.reshape(devices, slot_count * offloaded)], axis=1
    ).reshape(-1)
    row_weights = jnp.concatenate(
        [
            jnp.ones((devices, kept_count), jnp.float32),
            jnp.repeat(filled.astype(jnp.float32), offloaded, axis=1),
        ],
        axis=1,
    ).reshape(-1)
    my_grads = (
        lax.psum_scatter(
            jnp.take(local_grads, row_table, axis=0).astype(jnp.float32) * row_weights[:, None],
            "dp",
            scatter_dimension=0,
            tiled=True,
        )
        / devices
    )
    keep_grad = my_grads[:kept_count]
    slot_grad = my_grads[kept_count:].reshape(slot_count, offloaded, columns)
    partial_value = jnp.sum(my_grads * my_grads)
    grad_norm = jnp.sqrt(lax.psum(partial_value, ("tensor", "dp")))
    new_local = adam_update(local_master, local_moment, local_second, keep_grad)
    updated = adam_update(offload_master, offload_moment, offload_second, slot_grad)
    formers = (offload_master, offload_moment, offload_second)
    slot_mask = my_filled[:, None, None]
    new_off = tuple((jnp.where(slot_mask, updated[place], formers[place]) for place in range(3)))
    keep_bf = new_local[0].astype(jnp.bfloat16)
    slot_bf = new_off[0].astype(jnp.bfloat16)
    back_out = jnp.where(
        (owner_map == position)[:, None, None],
        jnp.take(slot_bf, slot_of, axis=0),
        jnp.zeros((), jnp.bfloat16),
    )
    back_in = lax.all_to_all(back_out, "dp", split_axis=0, concat_axis=0, tiled=True)
    mine_off = jnp.take(back_in, jnp.take(owner_map, position), axis=0)
    stacked = jnp.concatenate([keep_bf, mine_off], axis=0)
    order_rows = jnp.where(
        jnp.take(is_off, position, axis=0),
        kept_count + jnp.take(off_rank, position, axis=0),
        jnp.take(keep_rank, position, axis=0),
    )
    new_weights = lax.all_gather(jnp.take(stacked, order_rows, axis=0), "dp", axis=0, tiled=True)
    return (
        new_weights,
        grad_norm,
        new_local[0],
        new_local[1],
        new_local[2],
        new_off[0],
        new_off[1],
        new_off[2],
    )


def solution(mesh):
    return jax.shard_map(
        body,
        mesh=mesh,
        in_specs=(
            P("dp", None, "tensor"),
            P(),
            P(),
            P("dp", "tensor"),
            P("dp", "tensor"),
            P("dp", "tensor"),
            P("dp", None, "tensor"),
            P("dp", None, "tensor"),
            P("dp", None, "tensor"),
        ),
        out_specs=(
            P(None, "tensor"),
            P(),
            P("dp", "tensor"),
            P("dp", "tensor"),
            P("dp", "tensor"),
            P("dp", None, "tensor"),
            P("dp", None, "tensor"),
            P("dp", None, "tensor"),
        ),
        check_vma=False,
    )
```

profile of v0, /device:TPU:0, one launch (start us, length us, event | category | flops | bytes accessed | tf_op | source)
XLA Modules:
  0.0 106.5 jit_solution(14819365956823482855)
XLA Ops:
  0.6 0.9 convert_reduce_fusion
  1.6 0.7 iota_compare_fusion.2
  2.6 0.7 fusion.16
  3.3 0.8 reduce_window_sum.11
  4.1 0.7 iota_subtract_fusion
  5.1 0.6 gather_fusion
  7.0 1.1 gather_fusion.1
  8.1 0.2 convert_multiply_fusion
  8.3 26.0 %fusion = f32[8,7168]{1,0:T(8,128)S(1)} fusion(f32[56,7168]{1,0:T(8,128)S(1)} %convert_multiply_fusion), kind=kCustom, calls=%all-reduce-scatter | all-reduce-scatter fusion | flops 458753 | bytes 1835520
  34.4 1.4 %collective-permute-start = (f32[7,7168]{1,0:T(8,128)S(1)}, f32[7,7168]{1,0:T(8,128)S(1)}, u32[]{:S(2)}, u32[]{:S(2)}) collective-permute-start(f32[7,7168]{1,0:T(8,128)S(1)} %slice.53), channel_id=1, source_target_pairs={{0,1},{1,2},{2,3},{3,4},{4,5},{5,6},{6,7},{8,9},{9,10},{10,11},{11... | collective-permute-start | bytes 602120
  35.9 0.6 dynamic-slice.16
  36.5 0.2 select_reduce_fusion.1
  37.4 0.6 dynamic-slice.26
  38.7 0.4 concatenate.17
  39.1 0.7 multiply_reduce_fusion
  39.9 1.2 %fusion.15 = (bf16[2,2,7168]{2,1,0:T(2,128)(2,1)S(1)}, f32[2,2,7168]{2,1,0:T(2,128)}, f32[2,2,7168]{2,1,0:T(2,128)}, f32[2,2,7168]{2,1,0:T(2,128)}) fusion(f32[2,2,7168]{2,1,0:T(2,128)S(1)} %copy-done.1, f32[2,2,7168]{2,1,0:T(2,128)S(1)} %reshape.182, f32[2,2,7168]{2,1,0:T(2,128)S(1)} %copy-done.2, f32[2,2,7168]{2,1,0:T(2,128)S(1)} %copy-done.3, ...), kind=kLoop, calls=%fused_computation.71 | loop fusion | flops 544768 | bytes 860162 | tf_op jit(solution)/shard_map/convert_element_type | solution.py:104
  41.1 1.0 gather_fusion.2
  42.1 1.0 broadcast_select_fusion.1
  43.1 6.1 %all-to-all-start = ((bf16[8,2,7168]{2,1,0:T(2,128)(2,1)}), bf16[8,2,7168]{2,1,0:T(2,128)(2,1)S(1)}, u32[]{:S(2)}, u32[]{:S(2)}) async-start(bf16[8,2,7168]{2,1,0:T(2,128)(2,1)} %broadcast_select_fusion.1), calls=%async_computation | async-start | bytes 458752 | tf_op jit(solution)/shard_map/all_to_all | solution.py:110
  49.2 0.9 fusion.13
  50.1 41.1 %psum.7 = f32[]{:T(128)} all-reduce(f32[]{:T(128)} %get-tuple-element.64), channel_id=1, replica_groups=mesh['tensor'=4,'dp'=8] {'tensor','dp'}, use_global_device_ids=true, to_apply=%region_8.10 | all-reduce | flops 1 | bytes 8 | tf_op jit(solution)/shard_map/psum | solution.py:97
  92.0 0.6 gather_fusion.3
  92.7 11.6 %all-gather = bf16[8,5,7168]{2,1,0:T(8,128)(2,1)S(1)} all-gather(bf16[1,5,7168]{2,1,0:T(8,128)(2,1)S(1)} %select_bitcast_fusion), channel_id=1, replica_groups=mesh['tensor'=4,'dp'=8] {'dp'}, dimensions={0}, use_global_device_ids=true | all-gather | bytes 645120 | tf_op jit(solution)/shard_map/all_gather | solution.py:118
  104.3 1.1 %reshape.367 = bf16[40,7168]{1,0:T(8,128)(2,1)} reshape(bf16[8,5,7168]{2,1,0:T(8,128)(2,1)S(1)} %all-gather) | data formatting | bytes 1146880
  (66 shorter events, 2.3 us)
Async XLA Ops:
  0.6 6.4 %copy-start = (bf16[1,40,7168]{2,1,0:T(8,128)(2,1)S(1)}, bf16[1,40,7168]{2,1,0:T(8,128)(2,1)}, u32[]{:S(2)}) copy-start(bf16[1,40,7168]{2,1,0:T(8,128)(2,1)} %param.11) | copy-start | bytes 1720324
  8.3 27.6 %copy-start.7 = (s32[8]{0:T(128)S(1)}, s32[8]{0:T(128)}, u32[]{:S(2)}) copy-start(s32[8]{0:T(128)} %param.13) | copy-start | bytes 100
  8.3 29.1 %copy-start.8 = (u32[32]{0:T(128)S(1)}, u32[32]{0:T(128)}, u32[]{:S(2)}) copy-start(u32[32]{0:T(128)} %constant.288) | copy-start | bytes 388
  34.3 5.5 %copy-start.1 = (f32[2,2,7168]{2,1,0:T(2,128)S(1)}, f32[2,2,7168]{2,1,0:T(2,128)}, u32[]{:S(2)}) copy-start(f32[2,2,7168]{2,1,0:T(2,128)} %param.17) | copy-start | bytes 344068
  34.4 5.5 %copy-start.2 = (f32[2,2,7168]{2,1,0:T(2,128)S(1)}, f32[2,2,7168]{2,1,0:T(2,128)}, u32[]{:S(2)}) copy-start(f32[2,2,7168]{2,1,0:T(2,128)} %param.19) | copy-start | bytes 344068
  34.4 5.5 %copy-start.3 = (f32[2,2,7168]{2,1,0:T(2,128)S(1)}, f32[2,2,7168]{2,1,0:T(2,128)}, u32[]{:S(2)}) copy-start(f32[2,2,7168]{2,1,0:T(2,128)} %param.18) | copy-start | bytes 344068
  34.4 4.2 %collective-permute-start = (f32[7,7168]{1,0:T(8,128)S(1)}, f32[7,7168]{1,0:T(8,128)S(1)}, u32[]{:S(2)}, u32[]{:S(2)}) collective-permute-start(f32[7,7168]{1,0:T(8,128)S(1)} %slice.53), channel_id=1, source_target_pairs={{0,1},{1,2},{2,3},{3,4},{4,5},{5,6},{6,7},{8,9},{9,10},{10,11},{11... | collective-permute-start | bytes 602120
  39.0 10.2 %copy-start.4 = (f32[3,7168]{1,0:T(4,128)S(1)}, f32[3,7168]{1,0:T(4,128)}, u32[]{:S(2)}) copy-start(f32[3,7168]{1,0:T(4,128)} %param.14) | copy-start | bytes 258052
  39.0 10.2 %copy-start.5 = (f32[3,7168]{1,0:T(4,128)S(1)}, f32[3,7168]{1,0:T(4,128)}, u32[]{:S(2)}) copy-start(f32[3,7168]{1,0:T(4,128)} %param.15) | copy-start | bytes 258052
  39.0 10.2 %copy-start.6 = (f32[3,7168]{1,0:T(4,128)S(1)}, f32[3,7168]{1,0:T(4,128)}, u32[]{:S(2)}) copy-start(f32[3,7168]{1,0:T(4,128)} %param.16) | copy-start | bytes 258052
  43.1 48.8 %all-to-all-start = ((bf16[8,2,7168]{2,1,0:T(2,128)(2,1)}), bf16[8,2,7168]{2,1,0:T(2,128)(2,1)S(1)}, u32[]{:S(2)}, u32[]{:S(2)}) async-start(bf16[8,2,7168]{2,1,0:T(2,128)(2,1)} %broadcast_select_fusion.1), calls=%async_computation | async-start | bytes 458752 | tf_op jit(solution)/shard_map/all_to_all | solution.py:110
where the time goes:
time: 107 us
  blocking collectives  78.7 us (74%)
  other arithmetic  8.58 us (8%)
  starting transfers between devices  7.55 us (7%)
  local copies, waits for them, and re-layouts  7.5 us (7%)
  between operations  4.15 us (4%)
    psum x1, blocking collectives, body(): grad_norm = jnp.sqrt(lax.psum(partial_value, ('tensor', 'dp')))  41.1 us
    unnamed x1, blocking collectives  26 us
    all_gather x1, blocking collectives, body(): lax.all_gather(jnp.take(stacked, order_rows, axis=0), 'dp', axis=0, tiled...  11.6 us
    all_to_all x1, starting transfers between devices, body(): lax.all_to_all(back_out, 'dp', split_axis=0, concat_axis=0, tiled=True)  6.12 us
    unnamed x23, local copies, waits for them, and re-layouts  2.18 us
  transfers between devices with their start and end apart: 2, of which 0 were waited for; matrix products, arithmetic and copies ran while one was open for 2% of the time, Pallas kernels for 0%

commit v1 on v0

--- a/solution.py
+++ b/solution.py
@@ -115,7 +115,12 @@
         kept_count + jnp.take(off_rank, position, axis=0),
         jnp.take(keep_rank, position, axis=0),
     )
-    new_weights = lax.all_gather(jnp.take(stacked, order_rows, axis=0), "dp", axis=0, tiled=True)
+    new_weights = jnp.concatenate(
+        lax.all_to_all(
+            jnp.stack([jnp.take(stacked, order_rows, axis=0)] * lax.axis_size("dp")), "dp", 0, 0
+        ),
+        axis=0,
+    )
     return (
         new_weights,
         grad_norm,

time: 107 us -> 112 us (1.047)
  waiting for transfers between devices: 0.01 us -> 5.64 us
  blocking collectives: 78.7 us -> 73.3 us
  starting transfers between devices: 7.55 us -> 11.1 us
    all_gather x1 -> x0, blocking collectives: 11.6 us -> none  [body(): lax.all_gather(jnp.take(stacked, order_rows, axis=0), 'dp', axis=0, tiled...]
    psum x1, blocking collectives: 41.1 us -> 47.3 us  [body(): grad_norm = jnp.sqrt(lax.psum(partial_value, ('tensor', 'dp')))]
    all_to_all x1, waiting for transfers between devices: 0.01 us -> 5.63 us  [body(): lax.all_to_all(back_out, 'dp', split_axis=0, concat_axis=0, tiled=True)]
    all_to_all x0 -> x1, starting transfers between devices: none -> 3.55 us  [body(): lax.all_to_all(jnp.stack([jnp.take(stacked, order_rows, axis=0)] * lax.ax...]
  transfers between devices with their start and end apart: 2 -> 3, of which waited for: 0 -> 1; matrix products, arithmetic and copies ran while one was open for 2% -> 2% of each run, Pallas kernels for 0% -> 0%
where the time goes in v1:
time: 112 us; the launch traced here: 111 us
  blocking collectives  73.3 us (65%)
  starting transfers between devices  11.1 us (10%)
  other arithmetic  8.57 us (8%)
  local copies, waits for them, and re-layouts  8.49 us (8%)
  waiting for transfers between devices  5.64 us (5%)
  between operations  4.14 us (4%)
    psum x1, blocking collectives, body(): grad_norm = jnp.sqrt(lax.psum(partial_value, ('tensor', 'dp')))  47.3 us
    unnamed x1, blocking collectives  26 us
    all_to_all x1, starting transfers between devices, body(): lax.all_to_all(back_out, 'dp', split_axis=0, concat_axis=0, tiled=True)  6.13 us
    all_to_all x1, waiting for transfers between devices, body(): lax.all_to_all(back_out, 'dp', split_axis=0, concat_axis=0, tiled=True)  5.63 us
    all_to_all x1, starting transfers between devices, body(): lax.all_to_all(jnp.stack([jnp.take(stacked, order_rows, axis=0)] * lax.ax...  3.55 us
  transfers between devices with their start and end apart: 3, of which 1 were waited for; matrix products, arithmetic and copies ran while one was open for 2% of the time, Pallas kernels for 0%

profile of v1, /device:TPU:0, one launch (start us, length us, event | category | flops | bytes accessed | tf_op | source)
XLA Modules:
  0.0 111.3 jit_solution(13649930519242615180)
XLA Ops:
  0.7 0.9 convert_reduce_fusion
  1.6 0.7 iota_compare_fusion.2
  2.7 0.7 fusion.16
  3.8 0.8 reduce_window_sum.11
  4.7 0.7 iota_subtract_fusion
  5.6 0.6 gather_fusion
  7.0 1.1 gather_fusion.1
  8.3 26.0 %fusion = f32[8,7168]{1,0:T(8,128)S(1)} fusion(f32[56,7168]{1,0:T(8,128)S(1)} %convert_multiply_fusion), kind=kCustom, calls=%all-reduce-scatter | all-reduce-scatter fusion | flops 458753 | bytes 1835520
  34.4 1.4 %collective-permute-start = (f32[7,7168]{1,0:T(8,128)S(1)}, f32[7,7168]{1,0:T(8,128)S(1)}, u32[]{:S(2)}, u32[]{:S(2)}) collective-permute-start(f32[7,7168]{1,0:T(8,128)S(1)} %slice.53), channel_id=1, source_target_pairs={{0,1},{1,2},{2,3},{3,4},{4,5},{5,6},{6,7},{8,9},{9,10},{10,11},{11... | collective-permute-start | bytes 602120
  35.9 0.6 dynamic-slice.16
  37.4 0.6 dynamic-slice.26
  38.6 0.4 concatenate.17
  39.0 0.7 multiply_reduce_fusion
  39.9 1.2 %fusion.15 = (bf16[2,2,7168]{2,1,0:T(2,128)(2,1)S(1)}, f32[2,2,7168]{2,1,0:T(2,128)}, f32[2,2,7168]{2,1,0:T(2,128)}, f32[2,2,7168]{2,1,0:T(2,128)}) fusion(f32[2,2,7168]{2,1,0:T(2,128)S(1)} %copy-done.1, f32[2,2,7168]{2,1,0:T(2,128)S(1)} %reshape.193, f32[2,2,7168]{2,1,0:T(2,128)S(1)} %copy-done.2, f32[2,2,7168]{2,1,0:T(2,128)S(1)} %copy-done.3, ...), kind=kLoop, calls=%fused_computation.71 | loop fusion | flops 544768 | bytes 860162 | tf_op jit(solution)/shard_map/convert_element_type | solution.py:104
  41.0 1.0 gather_fusion.2
  42.1 1.0 broadcast_select_fusion.1
  43.0 6.1 %all-to-all-start = ((bf16[8,2,7168]{2,1,0:T(2,128)(2,1)}), bf16[8,2,7168]{2,1,0:T(2,128)(2,1)S(1)}, u32[]{:S(2)}, u32[]{:S(2)}) async-start(bf16[8,2,7168]{2,1,0:T(2,128)(2,1)} %broadcast_select_fusion.1), calls=%async_computation | async-start | bytes 458752 | tf_op jit(solution)/shard_map/all_to_all | solution.py:110
  49.2 0.9 fusion.13
  50.1 5.6 %all-to-all-done = bf16[8,2,7168]{2,1,0:T(2,128)(2,1)S(1)} async-done(((bf16[8,2,7168]{2,1,0:T(2,128)(2,1)}), bf16[8,2,7168]{2,1,0:T(2,128)(2,1)S(1)}, u32[]{:S(2)}, u32[]{:S(2)}) %all-to-all-start) | async-done | bytes 229408 | tf_op jit(solution)/shard_map/all_to_all | solution.py:110
  55.8 0.6 gather_fusion.3
  56.5 1.0 stack.2
  57.5 3.6 %all-to-all-start.1 = ((bf16[8,5,7168]{2,1,0:T(8,128)(2,1)}), bf16[8,5,7168]{2,1,0:T(8,128)(2,1)S(1)}, u32[]{:S(2)}, u32[]{:S(2)}) async-start(bf16[8,5,7168]{2,1,0:T(8,128)(2,1)} %stack.2), calls=%async_computation.1 | async-start | bytes 1835008 | tf_op jit(solution)/shard_map/all_to_all | solution.py:119
  61.1 47.3 %psum.7 = f32[]{:T(128)} all-reduce(f32[]{:T(128)} %get-tuple-element.64), channel_id=1, replica_groups=mesh['tensor'=4,'dp'=8] {'tensor','dp'}, use_global_device_ids=true, to_apply=%region_8.10 | all-reduce | flops 1 | bytes 8 | tf_op jit(solution)/shard_map/psum | solution.py:97
  109.1 1.1 reshape.194
  (68 shorter events, 2.7 us)
Async XLA Ops:
  0.6 6.4 %copy-start = (bf16[1,40,7168]{2,1,0:T(8,128)(2,1)S(1)}, bf16[1,40,7168]{2,1,0:T(8,128)(2,1)}, u32[]{:S(2)}) copy-start(bf16[1,40,7168]{2,1,0:T(8,128)(2,1)} %param.11) | copy-start | bytes 1720324
  8.3 27.6 %copy-start.7 = (s32[8]{0:T(128)S(1)}, s32[8]{0:T(128)}, u32[]{:S(2)}) copy-start(s32[8]{0:T(128)} %param.13) | copy-start | bytes 100
  8.3 29.1 %copy-start.8 = (u32[32]{0:T(128)S(1)}, u32[32]{0:T(128)}, u32[]{:S(2)}) copy-start(u32[32]{0:T(128)} %constant.288) | copy-start | bytes 388
  34.3 5.5 %copy-start.1 = (f32[2,2,7168]{2,1,0:T(2,128)S(1)}, f32[2,2,7168]{2,1,0:T(2,128)}, u32[]{:S(2)}) copy-start(f32[2,2,7168]{2,1,0:T(2,128)} %param.17) | copy-start | bytes 344068
  34.4 5.5 %copy-start.2 = (f32[2,2,7168]{2,1,0:T(2,128)S(1)}, f32[2,2,7168]{2,1,0:T(2,128)}, u32[]{:S(2)}) copy-start(f32[2,2,7168]{2,1,0:T(2,128)} %param.19) | copy-start | bytes 344068
  34.4 5.5 %copy-start.3 = (f32[2,2,7168]{2,1,0:T(2,128)S(1)}, f32[2,2,7168]{2,1,0:T(2,128)}, u32[]{:S(2)}) copy-start(f32[2,2,7168]{2,1,0:T(2,128)} %param.18) | copy-start | bytes 344068
  34.4 4.2 %collective-permute-start = (f32[7,7168]{1,0:T(8,128)S(1)}, f32[7,7168]{1,0:T(8,128)S(1)}, u32[]{:S(2)}, u32[]{:S(2)}) collective-permute-start(f32[7,7168]{1,0:T(8,128)S(1)} %slice.53), channel_id=1, source_target_pairs={{0,1},{1,2},{2,3},{3,4},{4,5},{5,6},{6,7},{8,9},{9,10},{10,11},{11... | collective-permute-start | bytes 602120
  39.0 10.2 %copy-start.4 = (f32[3,7168]{1,0:T(4,128)S(1)}, f32[3,7168]{1,0:T(4,128)}, u32[]{:S(2)}) copy-start(f32[3,7168]{1,0:T(4,128)} %param.14) | copy-start | bytes 258052
  39.0 10.2 %copy-start.5 = (f32[3,7168]{1,0:T(4,128)S(1)}, f32[3,7168]{1,0:T(4,128)}, u32[]{:S(2)}) copy-start(f32[3,7168]{1,0:T(4,128)} %param.15) | copy-start | bytes 258052
  39.0 10.2 %copy-start.6 = (f32[3,7168]{1,0:T(4,128)S(1)}, f32[3,7168]{1,0:T(4,128)}, u32[]{:S(2)}) copy-start(f32[3,7168]{1,0:T(4,128)} %param.16) | copy-start | bytes 258052
  43.0 12.7 %all-to-all-start = ((bf16[8,2,7168]{2,1,0:T(2,128)(2,1)}), bf16[8,2,7168]{2,1,0:T(2,128)(2,1)S(1)}, u32[]{:S(2)}, u32[]{:S(2)}) async-start(bf16[8,2,7168]{2,1,0:T(2,128)(2,1)} %broadcast_select_fusion.1), calls=%async_computation | async-start | bytes 458752 | tf_op jit(solution)/shard_map/all_to_all | solution.py:110
  57.5 51.6 %all-to-all-start.1 = ((bf16[8,5,7168]{2,1,0:T(8,128)(2,1)}), bf16[8,5,7168]{2,1,0:T(8,128)(2,1)S(1)}, u32[]{:S(2)}, u32[]{:S(2)}) async-start(bf16[8,5,7168]{2,1,0:T(8,128)(2,1)} %stack.2), calls=%async_computation.1 | async-start | bytes 1835008 | tf_op jit(solution)/shard_map/all_to_all | solution.py:119
